TPU v7x, 32 devices: a whole 2x2x4 slice. The times are simulated.
32 devices in a mesh: groups: 2 (over x), ep: 8 (over z, y), node: 2 (over core).
Axes of the slice: x: 2, y: 2, z: 4, core: 2. Of those that a mesh axis runs over, the one named last changes fastest.
Arguments:
- tokens: bfloat16 [1024, 7168], P(('groups', 'ep', 'node')), parts along dimension 0, may hold values from -6 to 6
- expert_ids: int32 [1024, 8], P(('groups', 'ep', 'node')), parts along dimension 0, may hold values from 0 to 15, all different within a row; in each aligned block of 32 rows (0 to 31, 32 to 63, ...) at most 32 rows name the same one
- gate_weights: float32 [1024, 8], P(('groups', 'ep', 'node')), parts along dimension 0, may hold values from 0.05 to 0.5
- gate_up_weight: bfloat16 [16, 7168, 512], P(('ep', 'node')), may hold values from -0.0625 to 0.0625
- down_weight: bfloat16 [16, 256, 7168], P(('ep', 'node')), may hold values from -0.375 to 0.375
Outputs:
- moe_out: bfloat16 [1024, 7168], P(('groups', 'ep', 'node')), parts along dimension 0
There are 2 independent parts, one for each index of `groups`. A program takes and returns all parts, laid end to end along the dimension named above; an argument that names none is the same for every part. Nothing has to cross between parts.
Inputs may be any that keep to these rules, and one draw needn't show every extreme that they name: `expert_ids`: each token names 8 different experts; among the 32 tokens of one device no expert is named by more than 32 of them, a bound that some block reaches.
All inputs are finite; a program needn't handle non-finite values.
Results may differ from a plain program's by a relative error of at most 0.0058.
Values may be sent and summed in bfloat16 or wider, within the bound.
A program may use at most 128 MiB of HBM per device.

v0:
```python
import jax
import jax.numpy as jnp
from jax import lax
from jax.sharding import PartitionSpec as P


def run_experts(received, gate_up_weight, down_weight):
    inner_width = down_weight.shape[1]
    slot_rows = received[:, 0].reshape(-1, received.shape[3])
    gate_up = jnp.dot(slot_rows, gate_up_weight[0], preferred_element_type=jnp.float32)
    hidden = (jax.nn.silu(gate_up[:, :inner_width]) * gate_up[:, inner_width:]).astype(jnp.bfloat16)
    product = jnp.dot(hidden, down_weight[0], preferred_element_type=jnp.float32).astype(
        jnp.bfloat16
    )
    results = [product.reshape(received.shape[0], received.shape[2], received.shape[3])]
    return jnp.stack(results, axis=1)


def on_device(tokens, expert_ids, gate_weights, gate_up_weight, down_weight):
    ep_size = lax.axis_size("ep")
    node_size = lax.axis_size("node")
    devices = ep_size * node_size
    local_count = gate_up_weight.shape[0]
    expert_total = devices * local_count
    token_count = tokens.shape[0]
    model_width = tokens.shape[1]
    top_count = expert_ids.shape[1]
    capacity = max(2, (2 * token_count * top_count + expert_total - 1) // expert_total)
    flat_ids = expert_ids.reshape(-1)
    one_hot = (flat_ids[:, None] == jnp.arange(expert_total, dtype=jnp.int32)[None, :]).astype(
        jnp.int32
    )
    slot_rank = jnp.sum(jnp.cumsum(one_hot, axis=0) * one_hot, axis=1) - 1
    slot_index = flat_ids * capacity + slot_rank
    sources = jnp.arange(token_count * top_count, dtype=jnp.int32) // top_count
    outgoing = (
        jnp.zeros((expert_total * capacity, model_width), jnp.bfloat16)
        .at[slot_index]
        .set(tokens[sources])
    )
    outgoing = outgoing.reshape(devices, local_count, capacity, model_width)
    answers = run_experts(
        lax.all_to_all(outgoing, ("ep", "node"), split_axis=0, concat_axis=0, tiled=True),
        gate_up_weight,
        down_weight,
    )
    returned = lax.all_to_all(answers, ("ep", "node"), split_axis=0, concat_axis=0, tiled=True)
    returned = returned.reshape(expert_total * capacity, model_width)
    picked = returned[slot_index].astype(jnp.float32).reshape(token_count, top_count, model_width)
    combined = jnp.sum(gate_weights[:, :, None] * picked, axis=1).astype(jnp.bfloat16)
    return combined


def solution(mesh):
    placed = (
        P(("groups", "ep", "node"), None),
        P(("groups", "ep", "node"), None),
        P(("groups", "ep", "node"), None),
        P(("ep", "node"), None, None),
        P(("ep", "node"), None, None),
    )
    return jax.shard_map(
        on_device,
        mesh=mesh,
        in_specs=placed,
        out_specs=P(("groups", "ep", "node"), None),
        check_vma=False,
    )
```

profile of v0, /device:TPU:15, one launch (start us, length us, event | category | flops | bytes accessed | tf_op | source)
XLA Modules:
  0.0 381.9 jit_solution(4174145105046865924)
XLA Ops:
  0.0 0.0 copy-start
  0.0 0.8 copy.14
  0.8 0.1 eq.29
  0.9 0.1 eq.25
  1.0 0.7 broadcast_multiply_fusion
  1.7 0.6 reduce-window.6
  2.3 0.2 slice_reduce_fusion
  2.5 0.1 fusion.11
  2.6 0.1 copy.13
  2.7 0.1 mul.33
  2.8 0.0 copy-done
  2.8 20.2 %scatter_custom_fusion = bf16[512,7168]{1,0:T(8,128)(2,1)} fusion(s32[256]{0:T(256)S(1)} %bitcast.37, bf16[32,7168]{1,0:T(8,128)(2,1)S(1)} %copy-done, s32[1024]{0:T(1024)S(1)} %pad_clamp_fusion.1, bf16[]{:T(256)} %constant.27.clone.1), kind=kCustom, calls=%fused_computation.9 | custom fusion | bytes 7340034 | tf_op jit(solution)/shard_map/scatter | solution.py:39
  23.1 0.0 copy-start.3
  23.1 166.4 %all_to_all.10 = bf16[16,1,32,7168]{3,2,1,0:T(8,128)(2,1)S(1)} all-to-all(bf16[16,1,32,7168]{3,2,1,0:T(8,128)(2,1)} %bitcast.35), channel_id=1, replica_groups=mesh['groups'=2,'ep'=8,'node'=2] {'ep','node'}, dimensions={0} | all-to-all | bytes 14680064 | tf_op jit(solution)/shard_map/all_to_all | solution.py:43
  189.5 0.0 copy-done.3
  189.5 0.0 copy-start.1
  189.5 3.9 %fusion.1 = f32[512,512]{1,0:T(8,128)S(1)} fusion(bf16[512,7168]{1,0:T(8,128)(2,1)S(1)} %bitcast.36, bf16[1,7168,512]{2,1,0:T(8,128)(2,1)S(1)} %copy-done.3), kind=kOutput, calls=%fused_computation.6 | convolution fusion | flops 3758096384 | bytes 15728640 | tf_op jit(solution)/shard_map/dot_general | solution.py:10
  193.4 0.0 copy-done.1
  193.4 5.2 %convolution_convert_fusion = bf16[512,7168]{1,0:T(8,128)(2,1)} fusion(bf16[1,256,7168]{2,1,0:T(8,128)(2,1)S(1)} %copy-done.1, f32[512,512]{1,0:T(8,128)S(1)} %fusion.1), kind=kOutput, calls=%fused_computation.3 | convolution fusion | flops 1883504640 | bytes 12058624 | tf_op jit(solution)/shard_map/dot_general | solution.py:12
  198.6 0.0 copy-start.2
  198.6 5.9 %all-to-all-start.1 = ((bf16[16,1,32,7168]{3,2,1,0:T(8,128)(2,1)}), bf16[16,1,32,7168]{3,2,1,0:T(8,128)(2,1)}, u32[]{:S(2)}, u32[]{:S(2)}) async-start(bf16[16,1,32,7168]{3,2,1,0:T(8,128)(2,1)} %bitcast.34), calls=%async_computation.1 | async-start | bytes 14680064 | tf_op jit(solution)/shard_map/all_to_all | solution.py:47
  204.5 0.0 copy-done.2
  204.5 0.1 copy.12
  204.6 159.8 %all-to-all-done.1 = bf16[16,1,32,7168]{3,2,1,0:T(8,128)(2,1)} async-done(((bf16[16,1,32,7168]{3,2,1,0:T(8,128)(2,1)}), bf16[16,1,32,7168]{3,2,1,0:T(8,128)(2,1)}, u32[]{:S(2)}, u32[]{:S(2)}) %all-to-all-start.1) | async-done | bytes 7340064 | tf_op jit(solution)/shard_map/all_to_all | solution.py:47
  364.4 12.1 %gather_fusion = bf16[256,7168]{1,0:T(8,128)(2,1)} fusion(bf16[512,7168]{1,0:T(8,128)(2,1)} %bitcast.10, s32[1024]{0:T(1024)S(1)} %pad_clamp_fusion), kind=kCustom, calls=%fused_computation.1 | custom fusion | bytes 7341056 | tf_op jit(solution)/shard_map/gather | solution.py:49
  376.5 5.4 %fusion = bf16[32,7168]{1,0:T(8,128)(2,1)} fusion(bf16[256,7168]{1,0:T(8,128)(2,1)} %gather_fusion, f32[32,8]{1,0:T(8,128)S(1)} %copy.12), kind=kLoop, calls=%fused_computation.5 | loop fusion | flops 5275648 | bytes 4129792 | tf_op jit(solution)/shard_map/reduce_sum | solution.py:50
  (8 shorter events, 0.1 us)
Async XLA Ops:
  0.0 2.8 copy-start
  23.1 166.4 %copy-start.3 = (bf16[1,7168,512]{2,1,0:T(8,128)(2,1)S(1)}, bf16[1,7168,512]{2,1,0:T(8,128)(2,1)}, u32[]{:S(2)}) copy-start(bf16[1,7168,512]{2,1,0:T(8,128)(2,1)} %param.8) | copy-start | bytes 22020100
  189.5 3.9 %copy-start.1 = (bf16[1,256,7168]{2,1,0:T(8,128)(2,1)S(1)}, bf16[1,256,7168]{2,1,0:T(8,128)(2,1)}, u32[]{:S(2)}) copy-start(bf16[1,256,7168]{2,1,0:T(8,128)(2,1)} %param.9) | copy-start | bytes 11010052
  198.6 5.9 %copy-start.2 = (f32[32,8]{0,1:T(8,128)S(1)}, f32[32,8]{0,1:T(8,128)}, u32[]{:S(2)}) copy-start(f32[32,8]{0,1:T(8,128)} %param.7) | copy-start | bytes 3076
  198.6 165.8 %all-to-all-start.1 = ((bf16[16,1,32,7168]{3,2,1,0:T(8,128)(2,1)}), bf16[16,1,32,7168]{3,2,1,0:T(8,128)(2,1)}, u32[]{:S(2)}, u32[]{:S(2)}) async-start(bf16[16,1,32,7168]{3,2,1,0:T(8,128)(2,1)} %bitcast.34), calls=%async_computation.1 | async-start | bytes 14680064 | tf_op jit(solution)/shard_map/all_to_all | solution.py:47
where the time goes:
time: 382 us
  blocking collectives  166 us (43%)
  waiting for transfers between devices  160 us (42%)
  local copies, waits for them, and re-layouts  33.8 us (9%)
  matrix products  9.09 us (2%)
  other arithmetic  6.86 us (2%)
  starting transfers between devices  5.88 us (2%)
    all_to_all x1, blocking collectives, on_device(): lax.all_to_all(outgoing, ('ep', 'node'), split_axis=0, concat_axis=0, til...  166 us
    all_to_all x1, waiting for transfers between devices, on_device(): lax.all_to_all(answers, ('ep', 'node'), split_axis=0, concat_axis=0, tile...  160 us
    scatter x1, local copies, waits for them, and re-layouts, on_device(): outgoing = jnp.zeros((expert_total * capacity, model_width), jnp.bfloat16...  20.2 us
    gather x1, local copies, waits for them, and re-layouts, on_device(): returned[slot_index].astype(jnp.float32)  12.1 us
  transfers between devices with their start and end apart: 1, of which 1 were waited for; matrix products, arithmetic and copies ran while one was open for 0% of the time, Pallas kernels for 0%

commit v1 on v0

v1 whole, which is shorter than its diff:
```python
import jax
import jax.numpy as jnp
from jax import lax
from jax.sharding import PartitionSpec as P

AXES = ("ep", "node")


def on_device(tokens, expert_ids, gate_weights, gate_up_weight, down_weight):
    local_count, inner_width = down_weight.shape[0], down_weight.shape[1]
    device = lax.axis_index("ep") * lax.axis_size("node") + lax.axis_index("node")
    all_tokens = lax.all_gather(tokens, AXES, axis=0, tiled=True)
    all_ids = lax.all_gather(expert_ids, AXES, axis=0, tiled=True)
    all_weights = lax.all_gather(gate_weights, AXES, axis=0, tiled=True)
    total = 0.0
    for local in range(local_count):
        expert = device * local_count + local
        share = jnp.sum(jnp.where(all_ids == expert, all_weights, 0.0), axis=1)
        gate_up = jnp.dot(all_tokens, gate_up_weight[local], preferred_element_type=jnp.float32)
        hidden = (jax.nn.silu(gate_up[:, :inner_width]) * gate_up[:, inner_width:]).astype(
            jnp.bfloat16
        )
        product = jnp.dot(hidden, down_weight[local], preferred_element_type=jnp.float32)
        total = total + share[:, None] * product
    return lax.psum_scatter(total.astype(jnp.bfloat16), AXES, scatter_dimension=0, tiled=True)


def solution(mesh):
    placed = (
        P(("groups", "ep", "node"), None),
        P(("groups", "ep", "node"), None),
        P(("groups", "ep", "node"), None),
        P(("ep", "node"), None, None),
        P(("ep", "node"), None, None),
    )
    return jax.shard_map(
        on_device,
        mesh=mesh,
        in_specs=placed,
        out_specs=P(("groups", "ep", "node"), None),
        check_vma=False,
    )
```

time: 382 us -> 192 us (0.50)
  the two profiles are of different devices: /device:TPU:15 before, /device:TPU:0 now
where the time goes in v1:
time: 192 us; the launch traced here: 191 us
  waiting for transfers between devices  122 us (64%)
  blocking collectives  42.4 us (22%)
  matrix products  13.7 us (7%)
  between operations  13.4 us (7%)
    reduce_scatter x1, waiting for transfers between devices, on_device(): lax.psum_scatter(total.astype(jnp.bfloat16), AXES, scatter_dimension=0, t...  90.5 us
    all_gather x1, waiting for transfers between devices, on_device(): all_tokens = lax.all_gather(tokens, AXES, axis=0, tiled=True)  30.5 us
    all_gather x1, blocking collectives, on_device(): all_ids = lax.all_gather(expert_ids, AXES, axis=0, tiled=True)  24 us
    all_gather x1, blocking collectives, on_device(): all_weights = lax.all_gather(gate_weights, AXES, axis=0, tiled=True)  18.5 us
    dot_general x1, matrix products, on_device(): jnp.dot(all_tokens, gate_up_weight[local], preferred_element_type=jnp.flo...  8.58 us
    dot_general x1, matrix products, on_device(): jnp.dot(hidden, down_weight[local], preferred_element_type=jnp.float32)  5.1 us
  transfers between devices with their start and end apart: 2, of which 2 were waited for; matrix products, arithmetic and copies ran while one was open for 0% of the time, Pallas kernels for 0%

profile of v1, /device:TPU:0, one launch (start us, length us, event | category | flops | bytes accessed | tf_op | source)
XLA Modules:
  0.0 191.3 jit_solution(3483513615247243619)
XLA Ops:
  6.5 0.0 all-gather.4.cloned.1.call-start
  6.5 0.7 all-gather.4.cloned.1.call-update
  7.3 0.0 reduce-scatter.2.cloned.1.call-start
  7.3 24.0 %all-gather = s32[16,32,8]{1,2,0:T(8,128)S(1)} all-gather(s32[1,32,8]{1,2,0:T(8,128)} %bitcast.9), channel_id=1, replica_groups=mesh['groups'=2,'ep'=8,'node'=2] {'ep','node'}, dimensions={0}, use_global_device_ids=true | all-gather | bytes 17408 | tf_op jit(solution)/shard_map/all_gather | solution.py:13
  31.3 18.5 %all-gather.1 = f32[16,32,8]{1,2,0:T(8,128)S(1)} all-gather(f32[1,32,8]{1,2,0:T(8,128)} %bitcast.10), channel_id=1, replica_groups=mesh['groups'=2,'ep'=8,'node'=2] {'ep','node'}, dimensions={0}, use_global_device_ids=true | all-gather | bytes 17408 | tf_op jit(solution)/shard_map/all_gather | solution.py:14
  49.8 0.1 reshape.9
  49.8 30.5 %all-gather.4.cloned.1.call-done = bf16[512,7168]{1,0:T(8,128)(2,1)} async-done(((bf16[32,7168]{1,0:T(8,128)(2,1)}), bf16[512,7168]{1,0:T(8,128)(2,1)}) %all-gather.4.cloned.1.call-update) | async-done | bytes 7340048 | tf_op jit(solution)/shard_map/all_gather | solution.py:12
  80.3 0.0 copy-start
  80.3 8.6 %fusion = f32[512,512]{1,0:T(8,128)S(1)} fusion(bf16[512,7168]{1,0:T(8,128)(2,1)} %all-gather.4.cloned.1.call-done, bf16[1,7168,512]{2,1,0:T(8,128)(2,1)} %param.8), kind=kOutput, calls=%fused_computation.1 | convolution fusion | flops 3758096384 | bytes 15728640 | tf_op jit(solution)/shard_map/dot_general | solution.py:19
  88.9 0.0 copy-done
  88.9 5.1 %multiply_convert_fusion = bf16[512,7168]{1,0:T(8,128)(2,1)} fusion(f32[512]{0:T(512)S(1)} %reshape.9, bf16[1,256,7168]{2,1,0:T(8,128)(2,1)S(1)} %copy-done, f32[512,512]{1,0:T(8,128)S(1)} %fusion), kind=kOutput, calls=%fused_computation | convolution fusion | flops 1887174656 | bytes 12060672 | tf_op jit(solution)/shard_map/dot_general | solution.py:23
  94.0 0.0 reduce-scatter.2.cloned.1.call-update
  94.0 90.5 %reduce-scatter.2.cloned.1.call-done = bf16[32,7168]{1,0:T(8,128)(2,1)} async-done(((bf16[512,7168]{1,0:T(8,128)(2,1)}), bf16[32,7168]{1,0:T(8,128)(2,1)}) %reduce-scatter.2.cloned.1.call-update) | async-done | bytes 458768 | tf_op jit(solution)/shard_map/reduce_scatter | solution.py:25
  (1 shorter events, 0.0 us)
Async XLA Ops:
  6.5 73.8 %all-gather.4.cloned.1.call-start = ((), (), s32[]{:S(2)}) async-start(), calls=%async_computation.1 | async-start | bytes 7798784 | tf_op jit(solution)/shard_map/all_gather | solution.py:12
  7.3 177.3 %reduce-scatter.2.cloned.1.call-start = ((), (), s32[]{:S(2)}) async-start(), calls=%async_computation.2 | async-start | bytes 7798784 | tf_op jit(solution)/shard_map/reduce_scatter | solution.py:25
  80.3 8.6 %copy-start = (bf16[1,256,7168]{2,1,0:T(8,128)(2,1)S(1)}, bf16[1,256,7168]{2,1,0:T(8,128)(2,1)}, u32[]{:S(2)}) copy-start(bf16[1,256,7168]{2,1,0:T(8,128)(2,1)} %param.9) | copy-start | bytes 11010052
Sparse Core Ops, SparseCore 0:
  9.6 70.6 all-gather.3
  94.2 90.3 reduce-scatter.1

commit v2 on v1

--- a/solution.py
+++ b/solution.py
@@ -1,12 +1,21 @@
+import functools
+
 import jax
 import jax.numpy as jnp
 from jax import lax
+from jax.experimental import pallas as pl
+from jax.experimental.pallas import tpu as pltpu
 from jax.sharding import PartitionSpec as P
 
 AXES = ("ep", "node")
-
-
-def on_device(tokens, expert_ids, gate_weights, gate_up_weight, down_weight):
+PAIR = 2
+PIECES = 2
+LANES = 128
+VMEM_BYTES = 60 * 1024 * 1024
+MESH = pl.DeviceIdType.MESH
+
+
+def spread_out(tokens, expert_ids, gate_weights, gate_up_weight, down_weight):
     local_count, inner_width = down_weight.shape[0], down_weight.shape[1]
     device = lax.axis_index("ep") * lax.axis_size("node") + lax.axis_index("node")
     all_tokens = lax.all_gather(tokens, AXES, axis=0, tiled=True)
@@ -25,6 +34,325 @@
     return lax.psum_scatter(total.astype(jnp.bfloat16), AXES, scatter_dimension=0, tiled=True)
 
 
+def block_of(width, most):
+    return max(b for b in range(LANES, most + 1, LANES) if width % b == 0)
+
+
+def pick(table, z):
+    value = jnp.int32(table[0])
+    for k in range(1, len(table)):
+        value = jnp.where(z == k, jnp.int32(table[k]), value)
+    return value
+
+
+def near_first(z, line):
+    order = [z]
+    for d in range(1, line):
+        order += [j for j in (z - d, z + d) if 0 <= j < line]
+    return order
+
+
+def send_order(z, line):
+    order = near_first(z, line)
+    return order[1:2] + order[2:][::-1] + order[:1]
+
+
+def kernel(
+    line, experts, x_ref, wgu_hbm, wd_hbm, out_ref,
+    tok, part, near, chain, wg, wd, acc, hid,
+    x_sem, up_s, dn_s, y_s, tok_r, w_l, w_s, w_r, n_s, n_r, c_s, c_r,
+):
+    rows, width = out_ref.shape
+    inner = wd.shape[1]
+    e = lax.axis_index("ep")
+    c = lax.axis_index("node")
+    z, y = e // PAIR, e % PAIR
+    other = 1 - y
+    first, last = z == 0, z == line - 1
+    has_dn, has_up = z > 0, z < line - 1
+    to_up, to_dn = {"ep": e + PAIR}, {"ep": e - PAIR}
+    to_y, to_core = {"ep": z * PAIR + other}, {"node": 1 - c}
+
+    barrier = pltpu.get_barrier_semaphore()
+
+    def greet(target):
+        pl.semaphore_signal(barrier, inc=1, device_id=target, device_id_type=MESH)
+
+    greet(to_core)
+    greet(to_y)
+    pl.when(has_up)(lambda: greet(to_up))
+    pl.when(has_dn)(lambda: greet(to_dn))
+    pl.semaphore_wait(barrier, 2 + jnp.where(has_up, 1, 0) + jnp.where(has_dn, 1, 0))
+
+    def remote(src, dst, s, r, target):
+        return pltpu.make_async_remote_copy(
+            src_ref=src, dst_ref=dst, send_sem=s, recv_sem=r,
+            device_id=target, device_id_type=MESH,
+        )
+
+    def tok_copy(j, sems, target, own=False):
+        src = x_ref if own else tok.at[j, y]
+        return remote(src, tok.at[j, y], sems.at[j], tok_r.at[j, y], target)
+
+    def tok_arrived(j, row):
+        remote(tok.at[j, row], tok.at[j, row], up_s.at[j], tok_r.at[j, row], to_y).wait_recv()
+
+    def forward(d):
+        own = d == 0
+
+        def below():
+            j = z - d
+            if not own:
+                tok_arrived(j, y)
+            pl.when(has_up)(lambda: tok_copy(j, up_s, to_up, own).start())
+            if own:
+                pl.when(has_dn)(lambda: tok_copy(j, dn_s, to_dn, own).start())
+            tok_copy(j, y_s, to_y, own).start()
+
+        def above():
+            j = z + d
+            tok_arrived(j, y)
+            pl.when(has_dn)(lambda: tok_copy(j, dn_s, to_dn).start())
+            tok_copy(j, y_s, to_y).start()
+
+        if own:
+            below()
+        else:
+            pl.when(z >= d)(below)
+            pl.when(z + d < line)(above)
+
+    forward(0)
+    own_copy = pltpu.make_async_copy(x_ref, tok.at[z, y], x_sem)
+    own_copy.start()
+    local = [
+        pltpu.make_async_copy(wgu_hbm.at[0], wg.at[0], w_l.at[0]),
+        pltpu.make_async_copy(wd_hbm.at[0], wd.at[0], w_l.at[1]),
+    ]
+    swapped = [
+        remote(wgu_hbm.at[0], wg.at[1], w_s.at[0], w_r.at[0], to_core),
+        remote(wd_hbm.at[0], wd.at[1], w_s.at[1], w_r.at[1], to_core),
+    ]
+    for copy in swapped + local:
+        copy.start()
+
+    mine = e * 2 + c
+    names = (mine, e * 2 + 1 - c)
+    k_block, n_block = block_of(width, 1792), block_of(width, 1024)
+
+    def compute(p):
+        j = pick([near_first(k, line)[p] for k in range(line)], z)
+        tok_arrived(j, other)
+        if p == 0:
+            own_copy.wait()
+            local[0].wait()
+            swapped[0].wait_recv()
+        acc[...] = jnp.zeros_like(acc)
+
+        def up_step(k, carry):
+            at = pl.ds(pl.multiple_of(k * k_block, k_block), k_block)
+            block = tok[j, :, :, at].reshape(PAIR * rows, k_block)
+            for s in range(2):
+                acc[s] += jnp.dot(block, wg[s, at, :], preferred_element_type=jnp.float32)
+            return carry
+
+        lax.fori_loop(0, width // k_block, up_step, 0)
+        for s in range(2):
+            gate, up = acc[s, :, :inner], acc[s, :, inner:]
+            hid[s] = (jax.nn.silu(gate) * up).astype(jnp.bfloat16)
+        meta = tok[j, :, :, width:].astype(jnp.float32).reshape(PAIR * rows, -1)
+        lane = lax.broadcasted_iota(jnp.int32, meta.shape, 1)
+        shares = [
+            jnp.sum(
+                jnp.where((lane == name) | (lane == name + experts), meta, 0.0),
+                axis=1, keepdims=True,
+            )
+            for name in names
+        ]
+        if p == 0:
+            local[1].wait()
+            swapped[1].wait_recv()
+
+        def down_step(n, carry):
+            at = pl.ds(pl.multiple_of(n * n_block, n_block), n_block)
+            total = 0.0
+            for s in range(2):
+                total += shares[s] * jnp.dot(
+                    hid[s], wd[s, :, at], preferred_element_type=jnp.float32
+                )
+            part[j, :, :, at] = total.astype(jnp.bfloat16).reshape(PAIR, rows, n_block)
+            return carry
+
+        lax.fori_loop(0, width // n_block, down_step, 0)
+
+    piece = width // PIECES
+
+    def near_copy(j, q):
+        at = pl.ds(q * piece, piece)
+        return remote(
+            part.at[j, other, :, at], near.at[j, :, at], n_s.at[j, q], n_r.at[j, q], to_y
+        )
+
+    def send_near(p):
+        j = pick([send_order(k, line)[p] for k in range(line)], z)
+        for q in range(PIECES):
+            near_copy(j, q).start()
+
+    for d in range(1, line):
+        forward(d)
+        if d == line - 1:
+            break
+        compute(d - 1)
+    compute(line - 2)
+    send_near(0)
+    compute(line - 1)
+    for p in range(1, line):
+        send_near(p)
+
+    def chain_copy(j, slot, q, target):
+        at = pl.ds(q * piece, piece)
+        return remote(
+            part.at[j, y, :, at], chain.at[slot, :, at], c_s.at[j, q], c_r.at[slot, q], target
+        )
+
+    def chain_arrived(slot, q):
+        chain_copy(0, slot, q, to_y).wait_recv()
+
+    def chain_up(j, d, q, start):
+        copy = chain_copy(j, j, q, to_up)
+        copy.start() if start else copy.wait_send()
+
+    def chain_dn(j, d, q, start):
+        copy = chain_copy(j, line if d == 1 else j, q, to_dn)
+        copy.start() if start else copy.wait_send()
+
+    def hop(j, q, came, push):
+        at = pl.ds(q * piece, piece)
+        near_copy(j, q).wait_recv()
+        pl.when(came)(lambda: chain_arrived(j, q))
+        total = part[j, y, :, at].astype(jnp.float32) + near[j, :, at].astype(jnp.float32)
+
+        @pl.when(came)
+        def _():
+            part[j, y, :, at] = (total + chain[j, :, at].astype(jnp.float32)).astype(jnp.bfloat16)
+
+        @pl.when(jnp.logical_not(came))
+        def _():
+            part[j, y, :, at] = total.astype(jnp.bfloat16)
+
+        push()
+
+    for d in range(line - 1, 0, -1):
+        for q in range(PIECES):
+            pl.when(z + d < line)(functools.partial(
+                lambda d, q: hop(z + d, q, has_dn, lambda: chain_up(z + d, d, q, True)), d, q))
+            pl.when(z >= d)(functools.partial(
+                lambda d, q: hop(z - d, q, has_up, lambda: chain_dn(z - d, d, q, True)), d, q))
+
+    for q in range(PIECES):
+        at = pl.ds(q * piece, piece)
+        near_copy(z, q).wait_recv()
+        pl.when(has_dn)(lambda: chain_arrived(z, q))
+        pl.when(has_up)(lambda: chain_arrived(line, q))
+        total = part[z, y, :, at].astype(jnp.float32) + near[z, :, at].astype(jnp.float32)
+        below = chain[z, :, at].astype(jnp.float32)
+        above = chain[line, :, at].astype(jnp.float32)
+
+        @pl.when(has_dn & has_up)
+        def _():
+            out_ref[:, at] = (total + below + above).astype(jnp.bfloat16)
+
+        @pl.when(first)
+        def _():
+            out_ref[:, at] = (total + above).astype(jnp.bfloat16)
+
+        @pl.when(last)
+        def _():
+            out_ref[:, at] = (total + below).astype(jnp.bfloat16)
+
+    for copy in swapped:
+        copy.wait_send()
+    for d in range(line):
+        own = d == 0
+
+        def below(d=d, own=own):
+            pl.when(has_up)(lambda: tok_copy(z - d, up_s, to_up, own).wait_send())
+            if own:
+                pl.when(has_dn)(lambda: tok_copy(z, dn_s, to_dn, own).wait_send())
+            else:
+                for q in range(PIECES):
+                    chain_dn(z - d, d, q, False)
+            tok_copy(z - d, y_s, to_y, own).wait_send()
+            for q in range(PIECES):
+                near_copy(z - d, q).wait_send()
+
+        def above(d=d):
+            pl.when(has_dn)(lambda: tok_copy(z + d, dn_s, to_dn).wait_send())
+            tok_copy(z + d, y_s, to_y).wait_send()
+            for q in range(PIECES):
+                chain_up(z + d, d, q, False)
+                near_copy(z + d, q).wait_send()
+
+        if own:
+            below()
+        else:
+            pl.when(z >= d)(below)
+            pl.when(z + d < line)(above)
+
+
+def on_grid(line, tokens, expert_ids, gate_weights, gate_up_weight, down_weight):
+    experts = lax.axis_size("ep") * lax.axis_size("node")
+    rows, width = tokens.shape
+    inner = down_weight.shape[1]
+    chosen = expert_ids[:, :, None] == jnp.arange(experts, dtype=jnp.int32)
+    share = jnp.sum(jnp.where(chosen, gate_weights[:, :, None], 0.0), axis=1)
+    high = lax.reduce_precision(share, 8, 7)
+    tail = -2 * experts % LANES
+    rest = jnp.pad(jnp.concatenate([high, share - high], axis=1), ((0, 0), (0, tail)))
+    x = jnp.concatenate([tokens, rest.astype(jnp.bfloat16)], axis=1)
+    dma, vmem, bf = pltpu.SemaphoreType.DMA, pltpu.VMEM, jnp.bfloat16
+    return pl.pallas_call(
+        functools.partial(kernel, line, experts),
+        out_shape=jax.ShapeDtypeStruct((rows, width), bf),
+        in_specs=[
+            pl.BlockSpec(memory_space=pltpu.VMEM),
+            pl.BlockSpec(memory_space=pl.ANY),
+            pl.BlockSpec(memory_space=pl.ANY),
+        ],
+        out_specs=pl.BlockSpec(memory_space=pltpu.VMEM),
+        scratch_shapes=[
+            vmem((line, PAIR, rows, x.shape[1]), bf),
+            vmem((line, PAIR, rows, width), bf),
+            vmem((line, rows, width), bf),
+            vmem((line + 1, rows, width), bf),
+            vmem((2, width, 2 * inner), bf),
+            vmem((2, inner, width), bf),
+            vmem((2, PAIR * rows, 2 * inner), jnp.float32),
+            vmem((2, PAIR * rows, inner), bf),
+            dma(()), dma((line,)), dma((line,)), dma((line,)), dma((line, PAIR)),
+            dma((2,)), dma((2,)), dma((2,)),
+            dma((line, PIECES)), dma((line, PIECES)),
+            dma((line, PIECES)), dma((line + 1, PIECES)),
+        ],
+        compiler_params=pltpu.CompilerParams(
+            collective_id=0, has_side_effects=True, vmem_limit_bytes=VMEM_BYTES
+        ),
+    )(x, gate_up_weight, down_weight)
+
+
+def on_device(tokens, expert_ids, gate_weights, gate_up_weight, down_weight):
+    chips, cores = lax.axis_size("ep"), lax.axis_size("node")
+    line = chips // PAIR
+    rows, width = tokens.shape
+    inner = down_weight.shape[1]
+    planes = (5 * line + 2 * PAIR) * rows * width * 2 + 6 * inner * width * 2 * 1.1
+    args = (tokens, expert_ids, gate_weights, gate_up_weight, down_weight)
+    fits = planes < 0.9 * VMEM_BYTES and gate_up_weight.shape[0] == 1
+    paired = cores == 2 and lax.axis_size("groups") * PAIR == 4
+    if fits and paired and chips % PAIR == 0 and line > 1:
+        return on_grid(line, *args)
+    return spread_out(*args)
+
+
 def solution(mesh):
     placed = (
         P(("groups", "ep", "node"), None),

time: 192 us -> 100 us (0.52)
  waiting for transfers between devices: 122 us -> 0 us
  Pallas kernels: 0 us -> 95.6 us
  blocking collectives: 42.4 us -> 0 us
  matrix products: 13.7 us -> 0 us
  between operations: 13.4 us -> 0.02 us
  other arithmetic: 0.03 us -> 2.64 us
    pallas_call x0 -> x1, Pallas kernels: none -> 95.6 us  [on_grid(): pl.pallas_call(functools.partial(kernel, line, experts), out_shape=jax.Sh...]
    reduce_scatter x1 -> x0, waiting for transfers between devices: 90.5 us -> none  [on_device(): lax.psum_scatter(total.astype(jnp.bfloat16), AXES, scatter_dimension=0, t...]
    all_gather x2 -> x0, blocking collectives: 42.4 us -> none  [the longest x1 24 us: on_device(): all_ids = lax.all_gather(expert_ids, AXES, axis=0, tiled=True)]
    all_gather x1 -> x0, waiting for transfers between devices: 30.5 us -> none  [on_device(): all_tokens = lax.all_gather(tokens, AXES, axis=0, tiled=True)]
    dot_general x2 -> x0, matrix products: 13.7 us -> none  [the longest x1 8.58 us: on_device(): jnp.dot(all_tokens, gate_up_weight[local], preferred_element_type=jnp.flo...]
  transfers between devices with their start and end apart: 2 -> 0, of which waited for: 2 -> 0; matrix products, arithmetic and copies ran while one was open for 0% -> 0% of each run, Pallas kernels for 0% -> 0%
where the time goes in v2:
time: 100 us
  Pallas kernels  95.6 us (96%)
  other arithmetic  2.64 us (3%)
  local copies, waits for them, and re-layouts  1.96 us (2%)
    pallas_call x1, Pallas kernels, on_grid(): pl.pallas_call(functools.partial(kernel, line, experts), out_shape=jax.Sh...  95.6 us

profile of v2, /device:TPU:0, one launch (start us, length us, event | category | flops | bytes accessed | tf_op | source)
XLA Modules:
  0.0 100.2 jit_solution(10349995725645185956)
XLA Ops:
  0.0 0.7 select_reduce_fusion
  0.7 0.1 copy.11
  0.8 0.1 copy.10
  0.9 0.1 fusion.2
  1.0 1.8 %pad_maximum_fusion.x_ref = bf16[32,7296]{1,0:T(8,128)(2,1)} fusion(bf16[32,128]{1,0:T(8,128)(2,1)S(1)} %fusion.2, bf16[32,7168]{1,0:T(8,128)(2,1)} %param.5), kind=kLoop, calls=%fused_computation | loop fusion | flops 933888 | bytes 933888 | tf_op jit(solution)/shard_map/concatenate | solution.py:311
  2.8 95.6 %shard_map.55 = bf16[32,7168]{1,0:T(8,128)(2,1)} custom-call(bf16[32,7296]{1,0:T(8,128)(2,1)} %pad_maximum_fusion.x_ref, bf16[1,7168,512]{2,1,0:T(8,128)(2,1)} %wgu_hbm.1, bf16[1,256,7168]{2,1,0:T(8,128)(2,1)} %wd_hbm.1), custom_call_target="tpu_custom_call" | custom-call | tf_op jit(solution)/shard_map/pallas_call | solution.py:313
  98.4 1.8 %copy.14 = bf16[32,7168]{1,0:T(8,128)(2,1)} copy(bf16[32,7168]{1,0:T(8,128)(2,1)} %shard_map.55) | data formatting | bytes 917504
  (2 shorter events, 0.0 us)

commit v3 on v2

--- a/solution.py
+++ b/solution.py
@@ -10,6 +10,7 @@
 AXES = ("ep", "node")
 PAIR = 2
 PIECES = 2
+SIDE = 7
 LANES = 128
 VMEM_BYTES = 60 * 1024 * 1024
 MESH = pl.DeviceIdType.MESH
@@ -59,11 +60,14 @@
 
 def kernel(
     line, experts, x_ref, wgu_hbm, wd_hbm, out_ref,
-    tok, part, near, chain, wg, wd, acc, hid,
+    tok, part, near, chain, near_b, chain_b, wg, wd, acc, hid,
     x_sem, up_s, dn_s, y_s, tok_r, w_l, w_s, w_r, n_s, n_r, c_s, c_r,
+    up_b, dn_b, y_b, tok_b, nb_s, nb_r, cb_s, cb_r,
 ):
     rows, width = out_ref.shape
     inner = wd.shape[1]
+    main = width - near_b.shape[1]
+    side = pl.ds(main, width - main)
     e = lax.axis_index("ep")
     c = lax.axis_index("node")
     z, y = e // PAIR, e % PAIR
@@ -91,29 +95,54 @@
         )
 
     def tok_copy(j, sems, target, own=False):
-        src = x_ref if own else tok.at[j, y]
-        return remote(src, tok.at[j, y], sems.at[j], tok_r.at[j, y], target)
+        at = pl.ds(0, main)
+        src = x_ref.at[:, at] if own else tok.at[j, y, :, at]
+        return remote(src, tok.at[j, y, :, at], sems.at[j], tok_r.at[j, y], target)
 
     def tok_arrived(j, row):
-        remote(tok.at[j, row], tok.at[j, row], up_s.at[j], tok_r.at[j, row], to_y).wait_recv()
+        ref = tok.at[j, row, :, pl.ds(0, main)]
+        remote(ref, ref, up_s.at[j], tok_r.at[j, row], to_y).wait_recv()
+
+    def side_copy(j, row, sem, target, own=False):
+        at = pl.ds(main, x_ref.shape[1] - main)
+        src = x_ref.at[:, at] if own else tok.at[j, row, :, at]
+        return remote(src, tok.at[j, row, :, at], sem, tok_b.at[j, row], target)
+
+    def side_up(j, row, own=False):
+        return side_copy(j, row, up_b.at[j, row], to_up, own)
+
+    def side_dn(j, row, own=False):
+        return side_copy(j, row, dn_b.at[j, row], to_dn, own)
 
     def forward(d):
         own = d == 0
 
         def below():
             j = z - d
-            if not own:
+            if own:
+                side_copy(j, y, y_b, to_y, own).start()
+            else:
                 tok_arrived(j, y)
             pl.when(has_up)(lambda: tok_copy(j, up_s, to_up, own).start())
             if own:
                 pl.when(has_dn)(lambda: tok_copy(j, dn_s, to_dn, own).start())
             tok_copy(j, y_s, to_y, own).start()
+            for row in (y, other):
+                mine = own and row is y
+                if not mine:
+                    side_up(j, row).wait_recv()
+                pl.when(has_up)(lambda: side_up(j, row, mine).start())
+                if own:
+                    pl.when(has_dn)(lambda: side_dn(j, row, mine).start())
 
         def above():
             j = z + d
             tok_arrived(j, y)
             pl.when(has_dn)(lambda: tok_copy(j, dn_s, to_dn).start())
             tok_copy(j, y_s, to_y).start()
+            for row in (y, other):
+                side_dn(j, row).wait_recv()
+                pl.when(has_dn)(lambda: side_dn(j, row).start())
 
         if own:
             below()
@@ -121,7 +150,6 @@
             pl.when(z >= d)(below)
             pl.when(z + d < line)(above)
 
-    forward(0)
     own_copy = pltpu.make_async_copy(x_ref, tok.at[z, y], x_sem)
     own_copy.start()
     local = [
@@ -135,6 +163,7 @@
     for copy in swapped + local:
         copy.start()
 
+    forward(0)
     mine = e * 2 + c
     names = (mine, e * 2 + 1 - c)
     k_block, n_block = block_of(width, 1792), block_of(width, 1024)
@@ -184,7 +213,7 @@
 
         lax.fori_loop(0, width // n_block, down_step, 0)
 
-    piece = width // PIECES
+    piece = main // PIECES
 
     def near_copy(j, q):
         at = pl.ds(q * piece, piece)
@@ -241,6 +270,47 @@
 
         push()
 
+    def side_sum(j, row, d, came, upward, start):
+        slot = line if d == 1 and not upward else j
+        copy = remote(
+            part.at[j, row, :, side], chain_b.at[slot, row], cb_s.at[j, row],
+            cb_r.at[slot, row], to_up if upward else to_dn,
+        )
+        if not start:
+            copy.wait_send()
+            return
+
+        @pl.when(came)
+        def _():
+            side_arrived(j, row)
+            total = part[j, row, :, side].astype(jnp.float32)
+            total += chain_b[j, row].astype(jnp.float32)
+            part[j, row, :, side] = total.astype(jnp.bfloat16)
+
+        copy.start()
+
+    def side_arrived(slot, row):
+        ref = chain_b.at[slot, row]
+        remote(ref, ref, cb_s.at[0, row], cb_r.at[slot, row], to_y).wait_recv()
+
+    def side_total(row):
+        pl.when(has_dn)(lambda: side_arrived(z, row))
+        pl.when(has_up)(lambda: side_arrived(line, row))
+        below, above = chain_b[z, row].astype(jnp.float32), chain_b[line, row].astype(jnp.float32)
+        total = part[z, row, :, side].astype(jnp.float32)
+        return total + jnp.where(has_dn, below, 0.0) + jnp.where(has_up, above, 0.0)
+
+    side_near = remote(part.at[z, other, :, side], near_b, nb_s, nb_r, to_y)
+    for d in range(line - 1, 0, -1):
+        for row in range(PAIR):
+            pl.when(z + d < line)(functools.partial(
+                lambda d, row: side_sum(z + d, row, d, has_dn, True, True), d, row))
+            pl.when(z >= d)(functools.partial(
+                lambda d, row: side_sum(z - d, row, d, has_up, False, True), d, row))
+    part[z, other, :, side] = side_total(other).astype(jnp.bfloat16)
+    side_near.start()
+    side_total_own = side_total(y)
+
     for d in range(line - 1, 0, -1):
         for q in range(PIECES):
             pl.when(z + d < line)(functools.partial(
@@ -269,6 +339,11 @@
         def _():
             out_ref[:, at] = (total + below).astype(jnp.bfloat16)
 
+    side_near.wait_recv()
+    out_ref[:, side] = (side_total_own + near_b[...].astype(jnp.float32)).astype(jnp.bfloat16)
+
+    side_near.wait_send()
+    side_copy(z, y, y_b, to_y, True).wait_send()
     for copy in swapped:
         copy.wait_send()
     for d in range(line):
@@ -276,6 +351,12 @@
 
         def below(d=d, own=own):
             pl.when(has_up)(lambda: tok_copy(z - d, up_s, to_up, own).wait_send())
+            for row in range(PAIR):
+                pl.when(has_up)(lambda row=row: side_up(z - d, row).wait_send())
+                if own:
+                    pl.when(has_dn)(lambda row=row: side_dn(z, row).wait_send())
+                else:
+                    side_sum(z - d, row, d, None, False, False)
             if own:
                 pl.when(has_dn)(lambda: tok_copy(z, dn_s, to_dn, own).wait_send())
             else:
@@ -287,6 +368,9 @@
 
         def above(d=d):
             pl.when(has_dn)(lambda: tok_copy(z + d, dn_s, to_dn).wait_send())
+            for row in range(PAIR):
+                pl.when(has_dn)(lambda row=row: side_dn(z + d, row).wait_send())
+                side_sum(z + d, row, d, None, True, False)
             tok_copy(z + d, y_s, to_y).wait_send()
             for q in range(PIECES):
                 chain_up(z + d, d, q, False)
@@ -309,6 +393,8 @@
     tail = -2 * experts % LANES
     rest = jnp.pad(jnp.concatenate([high, share - high], axis=1), ((0, 0), (0, tail)))
     x = jnp.concatenate([tokens, rest.astype(jnp.bfloat16)], axis=1)
+    step = LANES * PIECES
+    side = width - (width - width // SIDE) // step * step
     dma, vmem, bf = pltpu.SemaphoreType.DMA, pltpu.VMEM, jnp.bfloat16
     return pl.pallas_call(
         functools.partial(kernel, line, experts),
@@ -322,8 +408,10 @@
         scratch_shapes=[
             vmem((line, PAIR, rows, x.shape[1]), bf),
             vmem((line, PAIR, rows, width), bf),
-            vmem((line, rows, width), bf),
-            vmem((line + 1, rows, width), bf),
+            vmem((line, rows, width - side), bf),
+            vmem((line + 1, rows, width - side), bf),
+            vmem((rows, side), bf),
+            vmem((line + 1, PAIR, rows, side), bf),
             vmem((2, width, 2 * inner), bf),
             vmem((2, inner, width), bf),
             vmem((2, PAIR * rows, 2 * inner), jnp.float32),
@@ -332,6 +420,8 @@
             dma((2,)), dma((2,)), dma((2,)),
             dma((line, PIECES)), dma((line, PIECES)),
             dma((line, PIECES)), dma((line + 1, PIECES)),
+            dma((line, PAIR)), dma((line, PAIR)), dma(()), dma((line, PAIR)),
+            dma(()), dma(()), dma((line, PAIR)), dma((line + 1, PAIR)),
         ],
         compiler_params=pltpu.CompilerParams(
             collective_id=0, has_side_effects=True, vmem_limit_bytes=VMEM_BYTES

time: 100 us -> 96.2 us (0.962)
  Pallas kernels: 95.6 us -> 91.3 us
    pallas_call x1, Pallas kernels: 95.6 us -> 91.3 us  [on_grid(): pl.pallas_call(functools.partial(kernel, line, experts), out_shape=jax.Sh...]
where the time goes in v3:
time: 96.2 us; the launch traced here: 95.9 us
  Pallas kernels  91.3 us (95%)
  other arithmetic  2.64 us (3%)
  local copies, waits for them, and re-layouts  1.96 us (2%)
    pallas_call x1, Pallas kernels, on_grid(): pl.pallas_call(functools.partial(kernel, line, experts), out_shape=jax.Sh...  91.3 us

profile of v3, /device:TPU:0, one launch (start us, length us, event | category | flops | bytes accessed | tf_op | source)
XLA Modules:
  0.0 95.9 jit_solution(6529663363388185857)
XLA Ops:
  0.0 0.7 select_reduce_fusion
  0.7 0.1 copy.11
  0.8 0.1 copy.10
  0.9 0.1 fusion.2
  1.0 1.8 %pad_maximum_fusion.x_ref = bf16[32,7296]{1,0:T(8,128)(2,1)} fusion(bf16[32,128]{1,0:T(8,128)(2,1)S(1)} %fusion.2, bf16[32,7168]{1,0:T(8,128)(2,1)} %param.5), kind=kLoop, calls=%fused_computation | loop fusion | flops 933888 | bytes 933888 | tf_op jit(solution)/shard_map/concatenate | solution.py:395
  2.8 91.3 %shard_map.55 = bf16[32,7168]{1,0:T(8,128)(2,1)} custom-call(bf16[32,7296]{1,0:T(8,128)(2,1)} %pad_maximum_fusion.x_ref, bf16[1,7168,512]{2,1,0:T(8,128)(2,1)} %wgu_hbm.1, bf16[1,256,7168]{2,1,0:T(8,128)(2,1)} %wd_hbm.1), custom_call_target="tpu_custom_call" | custom-call | tf_op jit(solution)/shard_map/pallas_call | solution.py:399
  94.1 1.8 %copy.14 = bf16[32,7168]{1,0:T(8,128)(2,1)} copy(bf16[32,7168]{1,0:T(8,128)(2,1)} %shard_map.55) | data formatting | bytes 917504
  (2 shorter events, 0.0 us)

commit v4 on v3

--- a/solution.py
+++ b/solution.py
@@ -9,7 +9,7 @@
 
 AXES = ("ep", "node")
 PAIR = 2
-PIECES = 2
+PIECES = 4
 SIDE = 7
 LANES = 128
 VMEM_BYTES = 60 * 1024 * 1024
@@ -55,7 +55,7 @@
 
 def send_order(z, line):
     order = near_first(z, line)
-    return order[1:2] + order[2:][::-1] + order[:1]
+    return order[1:] + order[:1]
 
 
 def kernel(
@@ -232,9 +232,10 @@
             break
         compute(d - 1)
     compute(line - 2)
-    send_near(0)
+    for p in range(line - 2):
+        send_near(p)
     compute(line - 1)
-    for p in range(1, line):
+    for p in range(line - 2, line):
         send_near(p)
 
     def chain_copy(j, slot, q, target):

time: 96.2 us -> 99.2 us (1.031)
  Pallas kernels: 91.3 us -> 94.2 us
    pallas_call x1, Pallas kernels: 91.3 us -> 94.2 us  [on_grid(): pl.pallas_call(functools.partial(kernel, line, experts), out_shape=jax.Sh...]
where the time goes in v4:
time: 99.2 us; the launch traced here: 98.8 us
  Pallas kernels  94.2 us (95%)
  other arithmetic  2.64 us (3%)
  local copies, waits for them, and re-layouts  1.96 us (2%)
    pallas_call x1, Pallas kernels, on_grid(): pl.pallas_call(functools.partial(kernel, line, experts), out_shape=jax.Sh...  94.2 us

profile of v4, /device:TPU:0, one launch (start us, length us, event | category | flops | bytes accessed | tf_op | source)
XLA Modules:
  0.0 98.8 jit_solution(12014448411901350671)
XLA Ops:
  0.0 0.7 select_reduce_fusion
  0.7 0.1 copy.11
  0.8 0.1 copy.10
  0.9 0.1 fusion.2
  1.0 1.8 %pad_maximum_fusion.x_ref = bf16[32,7296]{1,0:T(8,128)(2,1)} fusion(bf16[32,128]{1,0:T(8,128)(2,1)S(1)} %fusion.2, bf16[32,7168]{1,0:T(8,128)(2,1)} %param.5), kind=kLoop, calls=%fused_computation | loop fusion | flops 933888 | bytes 933888 | tf_op jit(solution)/shard_map/concatenate | solution.py:396
  2.8 94.2 %shard_map.55 = bf16[32,7168]{1,0:T(8,128)(2,1)} custom-call(bf16[32,7296]{1,0:T(8,128)(2,1)} %pad_maximum_fusion.x_ref, bf16[1,7168,512]{2,1,0:T(8,128)(2,1)} %wgu_hbm.1, bf16[1,256,7168]{2,1,0:T(8,128)(2,1)} %wd_hbm.1), custom_call_target="tpu_custom_call" | custom-call | tf_op jit(solution)/shard_map/pallas_call | solution.py:400
  97.0 1.8 %copy.14 = bf16[32,7168]{1,0:T(8,128)(2,1)} copy(bf16[32,7168]{1,0:T(8,128)(2,1)} %shard_map.55) | data formatting | bytes 917504
  (2 shorter events, 0.0 us)
